TPU v7x, 32 devices: a whole 2x2x4 slice. The times are simulated.
32 devices in a mesh: dp: 8 (over z, x), tensor: 4 (over y, core).
Axes of the slice: x: 2, y: 2, z: 4, core: 2. Of those that a mesh axis runs over, the one named last changes fastest.
Arguments:
- ranges: bfloat16 [10240, 2652], P('dp'), may hold values from 0.049804688 to 2
- pot: float32 [10240], P('dp'), may hold values from 0.1 to 1
- w_ranges: bfloat16 [2652, 2048], P(None, 'tensor'), may hold values from -0.125 to 0.125
- w_pot: float32 [2048], P('tensor'), may hold values from -5 to 5
- bias_one: float32 [2048], P('tensor'), may hold values from -1.5 to 1.5
- w_two: bfloat16 [2048, 2048], P('dp', 'tensor'), may hold values from -0.125 to 0.125
- bias_two: float32 [2048], P('tensor'), may hold values from -1.5 to 1.5
- w_three: bfloat16 [2048, 2048], P('dp', 'tensor'), may hold values from -0.125 to 0.125
- bias_three: float32 [2048], P('tensor'), may hold values from -1.5 to 1.5
- w_out: bfloat16 [2048, 2652], P(('dp', 'tensor')), may hold values from -0.1875 to 0.1875
- bias_out: float32 [2652], replicated, may hold values from -1.5 to 1.5
Outputs:
- hand_values: float32 [10240, 2652], P(('dp', 'tensor'))
All inputs are finite; a program needn't handle non-finite values.
Results may differ from a plain program's by a relative error of at most 0.0039.
Values may be sent and summed in bfloat16 or wider, within the bound.
A program may use at most 128 MiB of HBM per device.

v0:
```python
import jax
import jax.numpy as jnp
from jax import lax
from jax.sharding import PartitionSpec as P


def relu_round(pre):
    return jnp.maximum(pre, 0.0).astype(jnp.bfloat16)


def fold_rows(left, piece):
    return jnp.dot(left, piece, preferred_element_type=jnp.float32)


def local(
    ranges, pot, w_ranges, w_pot, bias_one, w_two, bias_two, w_three, bias_three, w_out, bias_out
):
    groups = lax.axis_size("tensor")
    position = lax.axis_index("tensor")
    states = ranges.shape[0]
    own_count = states // groups
    lowest = position * own_count
    own_ranges = lax.dynamic_slice_in_dim(ranges, lowest, own_count, 0)
    pre = jnp.dot(ranges, w_ranges, preferred_element_type=jnp.float32)
    hidden = relu_round(pre + pot[:, None] * w_pot[None, :] + bias_one[None, :])
    for weight, bias in ((w_two, bias_two), (w_three, bias_three)):
        whole = lax.all_gather(hidden, "tensor", axis=1, tiled=True)
        summed = fold_rows(whole, lax.all_gather(weight, "dp", axis=0, tiled=True))
        hidden = relu_round(summed + bias[None, :])
    own_hidden = lax.all_to_all(hidden, "tensor", split_axis=0, concat_axis=1, tiled=True)
    out_block = lax.all_gather(w_out, "tensor", axis=0, tiled=True)
    values = (
        fold_rows(own_hidden, lax.all_gather(out_block, "dp", axis=0, tiled=True))
        + bias_out[None, :]
    )
    weights = own_ranges.astype(jnp.float32)
    error = jnp.sum(weights * values, axis=1) / jnp.sum(weights, axis=1)
    return values - error[:, None]


def solution(mesh):
    in_specs = (
        P("dp", None),
        P("dp"),
        P(None, "tensor"),
        P("tensor"),
        P("tensor"),
        P("dp", "tensor"),
        P("tensor"),
        P("dp", "tensor"),
        P("tensor"),
        P(("dp", "tensor"), None),
        P(),
    )
    out_specs = P(("dp", "tensor"), None)
    return jax.shard_map(local, mesh=mesh, in_specs=in_specs, out_specs=out_specs, check_vma=False)
```

profile of v0, /device:TPU:0, one launch (start us, length us, event | category | flops | bytes accessed | tf_op | source)
XLA Modules:
  0.0 390.5 jit_solution(3218508177793755378)
XLA Ops:
  6.5 0.7 all-gather.9.cloned.1.call-update
  7.3 0.0 all-gather.7.cloned.1.call-start
  7.3 1.0 copy-done
  8.3 8.0 %fusion.5 = bf16[1280,512]{1,0:T(8,128)(2,1)} fusion(bf16[1280,2652]{0,1:T(8,128)(2,1)} %param.11, bf16[2652,512]{1,0:T(8,128)(2,1)S(1)} %copy-done, f32[512]{0:T(512)} %param.15, f32[512]{0:T(512)} %param.14, f32[1280]{0:T(1024)} %param.12), kind=kOutput, calls=%fused_computation.11 | convolution fusion | flops 3479306240 | bytes 10824704 | tf_op jit(solution)/shard_map/dot_general | solution.py:24
  16.4 0.0 all-gather.15.cloned.1.call-start
  16.4 0.7 all-gather.15.cloned.1.call-update
  17.2 0.5 all-gather.13.cloned.1.call-update
  17.7 0.0 all-gather.11.cloned.1.call-start
  17.7 43.6 %all-gather.9.cloned.1.call-done = bf16[2048,512]{1,0:T(8,128)(2,1)} async-done(((bf16[256,512]{1,0:T(8,128)(2,1)}), bf16[2048,512]{1,0:T(8,128)(2,1)}) %all-gather.9.cloned.1.call-update) | async-done | bytes 2097168 | tf_op jit(solution)/shard_map/all_gather | solution.py:28
  61.3 40.5 %all-gather.7.cloned.1.call-done = bf16[1280,2048]{1,0:T(8,128)(2,1)} async-done(((bf16[1280,512]{1,0:T(8,128)(2,1)}), bf16[1280,2048]{1,0:T(8,128)(2,1)}) %all-gather.7.cloned.1.call-update) | async-done | bytes 5242896 | tf_op jit(solution)/shard_map/all_gather | solution.py:27
  101.8 7.1 %fusion.6 = bf16[1280,512]{1,0:T(8,128)(2,1)} fusion(bf16[1280,2048]{1,0:T(8,128)(2,1)} %all-gather.7.cloned.1.call-done, bf16[2048,512]{1,0:T(8,128)(2,1)} %all-gather.9.cloned.1.call-done, f32[512]{0:T(512)S(1)} %copy-done.2), kind=kOutput, calls=%fused_computation.12 | convolution fusion | flops 2686320640 | bytes 8652800 | tf_op jit(solution)/shard_map/dot_general | solution.py:12
  109.0 0.0 all-gather.17.cloned.1.call-start
  109.0 12.9 %all-gather.15.cloned.1.call-done = bf16[256,2652]{1,0:T(8,128)(2,1)} async-done(((bf16[64,2652]{1,0:T(8,128)(2,1)}), bf16[256,2652]{1,0:T(8,128)(2,1)}) %all-gather.15.cloned.1.call-update) | async-done | bytes 1357840 | tf_op jit(solution)/shard_map/all_gather | solution.py:31
  122.0 51.1 %all-gather.13.cloned.1.call-done = bf16[2048,512]{1,0:T(8,128)(2,1)} async-done(((bf16[256,512]{1,0:T(8,128)(2,1)}), bf16[2048,512]{1,0:T(8,128)(2,1)}) %all-gather.13.cloned.1.call-update) | async-done | bytes 2097168 | tf_op jit(solution)/shard_map/all_gather | solution.py:28
  173.1 40.4 %all-gather.11.cloned.1.call-done = bf16[1280,2048]{1,0:T(8,128)(2,1)} async-done(((bf16[1280,512]{1,0:T(8,128)(2,1)}), bf16[1280,2048]{1,0:T(8,128)(2,1)}) %all-gather.11.cloned.1.call-update) | async-done | bytes 5242896 | tf_op jit(solution)/shard_map/all_gather | solution.py:27
  213.5 7.1 %fusion.7 = bf16[1280,512]{1,0:T(8,128)(2,1)} fusion(bf16[1280,2048]{1,0:T(8,128)(2,1)} %all-gather.11.cloned.1.call-done, bf16[2048,512]{1,0:T(8,128)(2,1)} %all-gather.13.cloned.1.call-done, f32[512]{0:T(512)S(1)} %copy-done.3), kind=kOutput, calls=%fused_computation.13 | convolution fusion | flops 2686320640 | bytes 8652800 | tf_op jit(solution)/shard_map/dot_general | solution.py:12
  220.6 4.6 %all-to-all-start = ((bf16[4,320,512]{2,1,0:T(8,128)(2,1)}), bf16[4,320,512]{2,1,0:T(8,128)(2,1)}, u32[]{:S(2)}, u32[]{:S(2)}) async-start(bf16[4,320,512]{2,1,0:T(8,128)(2,1)} %bitcast.12), calls=%async_computation | async-start | bytes 2621440 | tf_op jit(solution)/shard_map/all_to_all | solution.py:30
  225.1 4.6 %constant_dynamic-slice_fusion = bf16[320,2652]{0,1:T(8,128)(2,1)} fusion(bf16[1280,2652]{0,1:T(8,128)(2,1)} %param.11, s32[]{:T(128)S(6)} %select_n.3), kind=kLoop, calls=%fused_computation.15 | loop fusion | bytes 3394564 | tf_op jit(solution)/shard_map/dynamic_slice | solution.py:23
  229.7 4.0 %copy.17 = bf16[320,2652]{1,0:T(8,128)(2,1)} copy(bf16[320,2652]{0,1:T(8,128)(2,1)} %constant_dynamic-slice_fusion) | data formatting | bytes 3394560
  233.7 8.6 %all-to-all-done = bf16[4,320,512]{2,1,0:T(8,128)(2,1)} async-done(((bf16[4,320,512]{2,1,0:T(8,128)(2,1)}), bf16[4,320,512]{2,1,0:T(8,128)(2,1)}, u32[]{:S(2)}, u32[]{:S(2)}) %all-to-all-start) | async-done | bytes 1310752 | tf_op jit(solution)/shard_map/all_to_all | solution.py:30
  242.2 2.6 copy.18
  244.8 127.6 %all-gather.17.cloned.1.call-done = bf16[2048,2652]{1,0:T(8,128)(2,1)} async-done(((bf16[256,2652]{1,0:T(8,128)(2,1)}), bf16[2048,2652]{1,0:T(8,128)(2,1)}) %all-gather.17.cloned.1.call-update) | async-done | bytes 10862608 | tf_op jit(solution)/shard_map/all_gather | solution.py:33
  372.4 9.1 %convert_reduce_fusion = (f32[320]{0:T(512)S(1)}, f32[320]{0:T(512)S(1)}, f32[320,2652]{1,0:T(8,128)S(1)}) fusion(bf16[320,2652]{1,0:T(8,128)(2,1)} %copy.17, f32[2652]{0:T(1024)S(1)} %copy-done.1, bf16[320,2048]{1,0:T(8,128)(2,1)} %bitcast.13, bf16[2048,2652]{1,0:T(8,128)(2,1)} %all-gather.17.cloned.1.call-done), kind=kOutput, calls=%fused_computation | convolution fusion | flops 3480272128 | bytes 17278320 | tf_op jit(solution)/shard_map/dot_general | solution.py:12
  381.6 2.1 broadcast_subtract_fusion
  (13 shorter events, 0.1 us)
Async XLA Ops:
  6.5 1.8 copy-start
  6.5 54.8 %all-gather.9.cloned.1.call-start = ((), (), s32[]{:S(2)}) async-start(), calls=%async_computation.2 | async-start | bytes 2359296 | tf_op jit(solution)/shard_map/all_gather | solution.py:28
  7.3 94.6 %copy-start.2 = (f32[512]{0:T(512)S(1)}, f32[512]{0:T(512)}, u32[]{:S(2)}) copy-start(f32[512]{0:T(512)} %param.17) | copy-start | bytes 6148
  7.3 94.6 %all-gather.7.cloned.1.call-start = ((), (), s32[]{:S(2)}) async-start(), calls=%async_computation.1 | async-start | bytes 6553600 | tf_op jit(solution)/shard_map/all_gather | solution.py:27
  16.4 105.6 %all-gather.15.cloned.1.call-start = ((), (), s32[]{:S(2)}) async-start(), calls=%async_computation.5 | async-start | bytes 1720320 | tf_op jit(solution)/shard_map/all_gather | solution.py:31
  17.1 156.0 %all-gather.13.cloned.1.call-start = ((), (), s32[]{:S(2)}) async-start(), calls=%async_computation.4 | async-start | bytes 2359296 | tf_op jit(solution)/shard_map/all_gather | solution.py:28
  17.7 195.8 %all-gather.11.cloned.1.call-start = ((), (), s32[]{:S(2)}) async-start(), calls=%async_computation.3 | async-start | bytes 6553600 | tf_op jit(solution)/shard_map/all_gather | solution.py:27
  108.9 104.5 %copy-start.3 = (f32[512]{0:T(512)S(1)}, f32[512]{0:T(512)}, u32[]{:S(2)}) copy-start(f32[512]{0:T(512)} %param.19) | copy-start | bytes 6148
  109.0 263.5 %all-gather.17.cloned.1.call-start = ((), (), s32[]{:S(2)}) async-start(), calls=%async_computation.6 | async-start | bytes 12386304 | tf_op jit(solution)/shard_map/all_gather | solution.py:33
  220.6 21.7 %all-to-all-start = ((bf16[4,320,512]{2,1,0:T(8,128)(2,1)}), bf16[4,320,512]{2,1,0:T(8,128)(2,1)}, u32[]{:S(2)}, u32[]{:S(2)}) async-start(bf16[4,320,512]{2,1,0:T(8,128)(2,1)} %bitcast.12), calls=%async_computation | async-start | bytes 2621440 | tf_op jit(solution)/shard_map/all_to_all | solution.py:30
  229.7 142.7 %copy-start.1 = (f32[2652]{0:T(1024)S(1)}, f32[2652]{0:T(1024)}, u32[]{:S(2)}) copy-start(f32[2652]{0:T(1024)} %param.21) | copy-start | bytes 31828
Sparse Core Ops, SparseCore 0:
  9.5 51.7 all-gather.8
  62.9 38.9 all-gather.6
  103.4 18.5 all-gather.14
  124.0 49.0 all-gather.12
  174.5 38.9 all-gather.10
  215.5 156.8 all-gather.16
where the time goes:
time: 391 us; the launch traced here: 390 us
  waiting for transfers between devices  327 us (84%)
  matrix products  31.4 us (8%)
  between operations  13.5 us (3%)
  local copies, waits for them, and re-layouts  12.1 us (3%)
  starting transfers between devices  4.76 us (1%)
    all_gather x1, waiting for transfers between devices, local(): lax.all_gather(out_block, 'dp', axis=0, tiled=True)  128 us
    all_gather x2, waiting for transfers between devices, local(): summed = fold_rows(whole, lax.all_gather(weight, 'dp', axis=0, tiled=True))  94.6 us
    all_gather x2, waiting for transfers between devices, local(): whole = lax.all_gather(hidden, 'tensor', axis=1, tiled=True)  80.9 us
    dot_general x3, matrix products, fold_rows(): return jnp.dot(left, piece, preferred_element_type=jnp.float32)  23.3 us
    all_gather x1, waiting for transfers between devices, local(): out_block = lax.all_gather(w_out, 'tensor', axis=0, tiled=True)  12.9 us
    all_to_all x1, waiting for transfers between devices, local(): lax.all_to_all(hidden, 'tensor', split_axis=0, concat_axis=1, tiled=True)  8.56 us
    dot_general x1, matrix products, local(): pre = jnp.dot(ranges, w_ranges, preferred_element_type=jnp.float32)  8.04 us
  transfers between devices with their start and end apart: 7, of which 7 were waited for; matrix products, arithmetic and copies ran while one was open for 9% of the time, Pallas kernels for 0%

commit v1 on v0

--- a/solution.py
+++ b/solution.py
@@ -2,6 +2,16 @@
 import jax.numpy as jnp
 from jax import lax
 from jax.sharding import PartitionSpec as P
+
+
+def around_the_ring(x, axis, dim):
+    devices = lax.axis_size(axis)
+    block, blocks = (x, [x])
+    for _ in range(devices - 1):
+        block = lax.ppermute(block, axis, [(i, (i + 1) % devices) for i in range(devices)])
+        blocks.insert(0, block)
+    line = jnp.concatenate(blocks, axis=dim)
+    return jnp.roll(line, (lax.axis_index(axis) + 1) * x.shape[dim], axis=dim)
 
 
 def relu_round(pre):
@@ -24,7 +34,7 @@
     pre = jnp.dot(ranges, w_ranges, preferred_element_type=jnp.float32)
     hidden = relu_round(pre + pot[:, None] * w_pot[None, :] + bias_one[None, :])
     for weight, bias in ((w_two, bias_two), (w_three, bias_three)):
-        whole = lax.all_gather(hidden, "tensor", axis=1, tiled=True)
+        whole = around_the_ring(hidden, "tensor", 1)
         summed = fold_rows(whole, lax.all_gather(weight, "dp", axis=0, tiled=True))
         hidden = relu_round(summed + bias[None, :])
     own_hidden = lax.all_to_all(hidden, "tensor", split_axis=0, concat_axis=1, tiled=True)

time: 391 us -> 307 us (0.79)
  waiting for transfers between devices: 327 us -> 227 us
  matrix products: 31.4 us -> 42 us
  local copies, waits for them, and re-layouts: 12.1 us -> 17.8 us
    ppermute x0 -> x6, waiting for transfers between devices: none -> 94.9 us  [around_the_ring(): lax.ppermute(block, axis, [(i, (i + 1) % devices) for i in range(devices)])]
    all_gather x2, waiting for transfers between devices: 94.6 us -> 7.91 us  [local(): summed = fold_rows(whole, lax.all_gather(weight, 'dp', axis=0, tiled=True))]
    all_gather x2 -> x0, waiting for transfers between devices: 80.9 us -> none  [local(): whole = lax.all_gather(hidden, 'tensor', axis=1, tiled=True)]
    all_gather x1, waiting for transfers between devices: 128 us -> 91.3 us  [local(): lax.all_gather(out_block, 'dp', axis=0, tiled=True)]
    dot_general x3, matrix products: 23.3 us -> 35 us  [fold_rows(): return jnp.dot(left, piece, preferred_element_type=jnp.float32)]
    all_gather x1, waiting for transfers between devices: 12.9 us -> 21.4 us  [local(): out_block = lax.all_gather(w_out, 'tensor', axis=0, tiled=True)]
    unnamed x9 -> x17, local copies, waits for them, and re-layouts: 5 us -> 8.19 us
  transfers between devices with their start and end apart: 7 -> 11, of which waited for: 7 -> 10; matrix products, arithmetic and copies ran while one was open for 9% -> 15% of each run, Pallas kernels for 0% -> 0%
where the time goes in v1:
time: 307 us; the launch traced here: 306 us
  waiting for transfers between devices  227 us (74%)
  matrix products  42 us (14%)
  local copies, waits for them, and re-layouts  17.8 us (6%)
  between operations  13.2 us (4%)
  starting transfers between devices  4.67 us (2%)
    ppermute x6, waiting for transfers between devices, around_the_ring(): lax.ppermute(block, axis, [(i, (i + 1) % devices) for i in range(devices)])  94.9 us
    all_gather x1, waiting for transfers between devices, local(): lax.all_gather(out_block, 'dp', axis=0, tiled=True)  91.3 us
    dot_general x3, matrix products, fold_rows(): return jnp.dot(left, piece, preferred_element_type=jnp.float32)  35 us
    all_gather x1, waiting for transfers between devices, local(): out_block = lax.all_gather(w_out, 'tensor', axis=0, tiled=True)  21.4 us
    all_to_all x1, waiting for transfers between devices, local(): lax.all_to_all(hidden, 'tensor', split_axis=0, concat_axis=1, tiled=True)  9.15 us
    unnamed x17, local copies, waits for them, and re-layouts  8.19 us
    all_gather x2, waiting for transfers between devices, local(): summed = fold_rows(whole, lax.all_gather(weight, 'dp', axis=0, tiled=True))  7.91 us
    dot_general x1, matrix products, local(): pre = jnp.dot(ranges, w_ranges, preferred_element_type=jnp.float32)  6.99 us
  transfers between devices with their start and end apart: 11, of which 10 were waited for; matrix products, arithmetic and copies ran while one was open for 15% of the time, Pallas kernels for 0%

profile of v1, /device:TPU:0, one launch (start us, length us, event | category | flops | bytes accessed | tf_op | source)
XLA Modules:
  0.0 306.4 jit_solution(1768950720743668701)
XLA Ops:
  8.8 21.4 %all-gather.9.cloned.1.call-done = bf16[256,2652]{1,0:T(8,128)(2,1)} async-done(((bf16[64,2652]{1,0:T(8,128)(2,1)}), bf16[256,2652]{1,0:T(8,128)(2,1)}) %all-gather.9.cloned.1.call-update) | async-done | bytes 1357840 | tf_op jit(solution)/shard_map/all_gather | solution.py:41
  30.2 7.0 %fusion.39 = bf16[1280,512]{0,1:T(8,128)(2,1)S(1)} fusion(bf16[1280,2652]{0,1:T(8,128)(2,1)} %param.13, bf16[2652,512]{1,0:T(8,128)(2,1)S(1)} %copy-done, f32[512]{0:T(512)} %param.17, f32[512]{0:T(512)} %param.16, f32[1280]{0:T(1024)} %param.14), kind=kOutput, calls=%fused_computation.45 | convolution fusion | flops 3479306240 | bytes 10824704 | tf_op jit(solution)/shard_map/dot_general | solution.py:34
  37.2 1.0 copy-done.1
  38.5 16.8 %collective-permute-done = bf16[1280,512]{0,1:T(8,128)(2,1)S(1)} collective-permute-done((bf16[1280,512]{0,1:T(8,128)(2,1)S(1)}, bf16[1280,512]{0,1:T(8,128)(2,1)S(1)}, u32[]{:S(2)}, u32[]{:S(2)}) %collective-permute-start) | collective-permute-done | bytes 1310752 | tf_op jit(solution)/shard_map/ppermute | solution.py:11
  55.3 1.1 copy-done.2
  56.4 17.1 %collective-permute-done.1 = bf16[1280,512]{0,1:T(8,128)(2,1)} collective-permute-done((bf16[1280,512]{0,1:T(8,128)(2,1)S(1)}, bf16[1280,512]{0,1:T(8,128)(2,1)}, u32[]{:S(2)}, u32[]{:S(2)}) %collective-permute-start.1) | collective-permute-done | bytes 1310752 | tf_op jit(solution)/shard_map/ppermute | solution.py:11
  73.5 7.9 %all-gather.5.cloned.1.call-done = bf16[2048,512]{1,0:T(8,128)(2,1)} async-done(((bf16[256,512]{1,0:T(8,128)(2,1)}), bf16[2048,512]{1,0:T(8,128)(2,1)}) %all-gather.5.cloned.1.call-update) | async-done | bytes 2097168 | tf_op jit(solution)/shard_map/all_gather | solution.py:38
  81.4 9.4 %collective-permute-done.2 = bf16[1280,512]{0,1:T(8,128)(2,1)} collective-permute-done((bf16[1280,512]{0,1:T(8,128)(2,1)}, bf16[1280,512]{0,1:T(8,128)(2,1)}, u32[]{:S(2)}, u32[]{:S(2)}) %collective-permute-start.2) | collective-permute-done | bytes 1310752 | tf_op jit(solution)/shard_map/ppermute | solution.py:11
  90.9 12.5 %fusion.33 = bf16[1280,512]{0,1:T(8,128)(2,1)S(1)} fusion(bf16[2048,512]{1,0:T(8,128)(2,1)} %all-gather.5.cloned.1.call-done, s32[]{:T(128)S(6)} %select_n.17, bf16[1280,512]{0,1:T(8,128)(2,1)} %collective-permute-done.2, bf16[1280,512]{0,1:T(8,128)(2,1)} %collective-permute-done.1, bf16[1280,512]{0,1:T(8,128)(2,1)} %copy-done.2, ...), kind=kOutput, calls=%fused_computation.43 | convolution fusion | flops 2728263680 | bytes 8652804 | tf_op jit(solution)/shard_map/dot_general | solution.py:22
  103.4 1.0 copy-done.3
  104.4 17.0 %collective-permute-done.3 = bf16[1280,512]{0,1:T(8,128)(2,1)S(1)} collective-permute-done((bf16[1280,512]{0,1:T(8,128)(2,1)S(1)}, bf16[1280,512]{0,1:T(8,128)(2,1)S(1)}, u32[]{:S(2)}, u32[]{:S(2)}) %collective-permute-start.3) | collective-permute-done | bytes 1310752 | tf_op jit(solution)/shard_map/ppermute | solution.py:11
  121.5 1.1 copy-done.4
  122.5 17.1 %collective-permute-done.4 = bf16[1280,512]{0,1:T(8,128)(2,1)} collective-permute-done((bf16[1280,512]{0,1:T(8,128)(2,1)S(1)}, bf16[1280,512]{0,1:T(8,128)(2,1)}, u32[]{:S(2)}, u32[]{:S(2)}) %collective-permute-start.4) | collective-permute-done | bytes 1310752 | tf_op jit(solution)/shard_map/ppermute | solution.py:11
  139.7 17.3 %collective-permute-done.5 = bf16[1280,512]{0,1:T(8,128)(2,1)} collective-permute-done((bf16[1280,512]{0,1:T(8,128)(2,1)}, bf16[1280,512]{0,1:T(8,128)(2,1)}, u32[]{:S(2)}, u32[]{:S(2)}) %collective-permute-start.5) | collective-permute-done | bytes 1310752 | tf_op jit(solution)/shard_map/ppermute | solution.py:11
  157.0 13.4 %fusion.36 = bf16[1280,512]{0,1:T(8,128)(2,1)} fusion(bf16[2048,512]{1,0:T(8,128)(2,1)} %all-gather.7.cloned.1.call-done, s32[]{:T(128)S(6)} %select_n.17, bf16[1280,512]{0,1:T(8,128)(2,1)} %collective-permute-done.5, bf16[1280,512]{0,1:T(8,128)(2,1)} %collective-permute-done.4, bf16[1280,512]{0,1:T(8,128)(2,1)} %copy-done.4, ...), kind=kOutput, calls=%fused_computation.44 | convolution fusion | flops 2728263680 | bytes 8652804 | tf_op jit(solution)/shard_map/dot_general | solution.py:22
  170.4 2.4 copy.15
  172.8 4.3 %all-to-all-start = ((bf16[4,320,512]{2,1,0:T(8,128)(2,1)}), bf16[4,320,512]{2,1,0:T(8,128)(2,1)}, u32[]{:S(2)}, u32[]{:S(2)}) async-start(bf16[4,320,512]{2,1,0:T(8,128)(2,1)} %bitcast.10), calls=%async_computation | async-start | bytes 2621440 | tf_op jit(solution)/shard_map/all_to_all | solution.py:40
  177.1 4.2 %constant_dynamic-slice_fusion = bf16[320,2652]{0,1:T(8,128)(2,1)} fusion(bf16[1280,2652]{0,1:T(8,128)(2,1)} %param.13, s32[]{:T(128)S(6)} %select_n.13), kind=kLoop, calls=%fused_computation.49 | loop fusion | bytes 3394564 | tf_op jit(solution)/shard_map/dynamic_slice | solution.py:33
  181.3 4.0 %copy.19 = bf16[320,2652]{1,0:T(8,128)(2,1)} copy(bf16[320,2652]{0,1:T(8,128)(2,1)} %constant_dynamic-slice_fusion) | data formatting | bytes 3394560
  185.3 9.1 %all-to-all-done = bf16[4,320,512]{2,1,0:T(8,128)(2,1)} async-done(((bf16[4,320,512]{2,1,0:T(8,128)(2,1)}), bf16[4,320,512]{2,1,0:T(8,128)(2,1)}, u32[]{:S(2)}, u32[]{:S(2)}) %all-to-all-start) | async-done | bytes 1310752 | tf_op jit(solution)/shard_map/all_to_all | solution.py:40
  194.4 2.9 copy.20
  197.4 91.3 %all-gather.11.cloned.1.call-done = bf16[2048,2652]{1,0:T(8,128)(2,1)} async-done(((bf16[256,2652]{1,0:T(8,128)(2,1)}), bf16[2048,2652]{1,0:T(8,128)(2,1)}) %all-gather.11.cloned.1.call-update) | async-done | bytes 10862608 | tf_op jit(solution)/shard_map/all_gather | solution.py:43
  288.7 9.1 %convert_reduce_fusion = (f32[320]{0:T(512)S(1)}, f32[320]{0:T(512)S(1)}, f32[320,2652]{1,0:T(8,128)S(1)}) fusion(bf16[320,2652]{1,0:T(8,128)(2,1)} %copy.19, f32[2652]{0:T(1024)S(1)} %copy-done.5, bf16[320,2048]{1,0:T(8,128)(2,1)} %bitcast.11, bf16[2048,2652]{1,0:T(8,128)(2,1)} %all-gather.11.cloned.1.call-done), kind=kOutput, calls=%fused_computation.32 | convolution fusion | flops 3480272128 | bytes 17278320 | tf_op jit(solution)/shard_map/dot_general | solution.py:22
  297.8 2.1 broadcast_subtract_fusion
  (28 shorter events, 2.5 us)
Async XLA Ops:
  6.5 23.7 %copy-start = (bf16[2652,512]{1,0:T(8,128)(2,1)S(1)}, bf16[2652,512]{1,0:T(8,128)(2,1)}, u32[]{:S(2)}) copy-start(bf16[2652,512]{1,0:T(8,128)(2,1)} %param.15) | copy-start | bytes 8146948
  6.5 23.6 %all-gather.9.cloned.1.call-start = ((), (), s32[]{:S(2)}) async-start(), calls=%async_computation.3 | async-start | bytes 1720320 | tf_op jit(solution)/shard_map/all_gather | solution.py:41
  7.3 74.2 %all-gather.5.cloned.1.call-start = ((), (), s32[]{:S(2)}) async-start(), calls=%async_computation.1 | async-start | bytes 2359296 | tf_op jit(solution)/shard_map/all_gather | solution.py:38
  8.0 131.6 %all-gather.7.cloned.1.call-start = ((), (), s32[]{:S(2)}) async-start(), calls=%async_computation.2 | async-start | bytes 2359296 | tf_op jit(solution)/shard_map/all_gather | solution.py:38
  8.7 280.0 %all-gather.11.cloned.1.call-start = ((), (), s32[]{:S(2)}) async-start(), calls=%async_computation.4 | async-start | bytes 12386304 | tf_op jit(solution)/shard_map/all_gather | solution.py:43
  30.2 60.6 %copy-start.6 = (f32[512]{0:T(512)S(1)}, f32[512]{0:T(512)}, u32[]{:S(2)}) copy-start(f32[512]{0:T(512)} %param.19) | copy-start | bytes 6148
  37.2 1.1 copy-start.1
  38.3 17.0 %collective-permute-start = (bf16[1280,512]{0,1:T(8,128)(2,1)S(1)}, bf16[1280,512]{0,1:T(8,128)(2,1)S(1)}, u32[]{:S(2)}, u32[]{:S(2)}) collective-permute-start(bf16[1280,512]{0,1:T(8,128)(2,1)S(1)} %fusion.39), channel_id=1, source_target_pairs={{0,1},{1,2},{2,3},{3,0},{4,5},{5,6},{6,7},{7,4},{8,9},{9,10},{10,1... | collective-permute-start | bytes 3932168 | tf_op jit(solution)/shard_map/ppermute | solution.py:11
  55.3 1.1 copy-start.2
  56.4 17.1 %collective-permute-start.1 = (bf16[1280,512]{0,1:T(8,128)(2,1)S(1)}, bf16[1280,512]{0,1:T(8,128)(2,1)}, u32[]{:S(2)}, u32[]{:S(2)}) collective-permute-start(bf16[1280,512]{0,1:T(8,128)(2,1)S(1)} %collective-permute-done), channel_id=1, source_target_pairs={{0,1},{1,2},{2,3},{3,0},{4,5},{5,6},{6,7},{7,4},{8,9},{9,10},{10,1... | collective-permute-start | bytes 3932168 | tf_op jit(solution)/shard_map/ppermute | solution.py:11
  73.5 17.3 %collective-permute-start.2 = (bf16[1280,512]{0,1:T(8,128)(2,1)}, bf16[1280,512]{0,1:T(8,128)(2,1)}, u32[]{:S(2)}, u32[]{:S(2)}) collective-permute-start(bf16[1280,512]{0,1:T(8,128)(2,1)} %collective-permute-done.1), channel_id=1, source_target_pairs={{0,1},{1,2},{2,3},{3,0},{4,5},{5,6},{6,7},{7,4},{8,9},{9,10},{10,1... | collective-permute-start | bytes 3932168 | tf_op jit(solution)/shard_map/ppermute | solution.py:11
  73.5 83.5 %copy-start.7 = (f32[512]{0:T(512)S(1)}, f32[512]{0:T(512)}, u32[]{:S(2)}) copy-start(f32[512]{0:T(512)} %param.21) | copy-start | bytes 6148
  103.4 1.1 copy-start.3
  104.4 17.0 %collective-permute-start.3 = (bf16[1280,512]{0,1:T(8,128)(2,1)S(1)}, bf16[1280,512]{0,1:T(8,128)(2,1)S(1)}, u32[]{:S(2)}, u32[]{:S(2)}) collective-permute-start(bf16[1280,512]{0,1:T(8,128)(2,1)S(1)} %fusion.33), channel_id=1, source_target_pairs={{0,1},{1,2},{2,3},{3,0},{4,5},{5,6},{6,7},{7,4},{8,9},{9,10},{10,1... | collective-permute-start | bytes 3932168 | tf_op jit(solution)/shard_map/ppermute | solution.py:11
  121.5 1.1 copy-start.4
  122.5 17.1 %collective-permute-start.4 = (bf16[1280,512]{0,1:T(8,128)(2,1)S(1)}, bf16[1280,512]{0,1:T(8,128)(2,1)}, u32[]{:S(2)}, u32[]{:S(2)}) collective-permute-start(bf16[1280,512]{0,1:T(8,128)(2,1)S(1)} %collective-permute-done.3), channel_id=1, source_target_pairs={{0,1},{1,2},{2,3},{3,0},{4,5},{5,6},{6,7},{7,4},{8,9},{9,10},{10,1... | collective-permute-start | bytes 3932168 | tf_op jit(solution)/shard_map/ppermute | solution.py:11
  139.6 17.3 %collective-permute-start.5 = (bf16[1280,512]{0,1:T(8,128)(2,1)}, bf16[1280,512]{0,1:T(8,128)(2,1)}, u32[]{:S(2)}, u32[]{:S(2)}) collective-permute-start(bf16[1280,512]{0,1:T(8,128)(2,1)} %collective-permute-done.4), channel_id=1, source_target_pairs={{0,1},{1,2},{2,3},{3,0},{4,5},{5,6},{6,7},{7,4},{8,9},{9,10},{10,1... | collective-permute-start | bytes 3932168 | tf_op jit(solution)/shard_map/ppermute | solution.py:11
  172.8 21.6 %all-to-all-start = ((bf16[4,320,512]{2,1,0:T(8,128)(2,1)}), bf16[4,320,512]{2,1,0:T(8,128)(2,1)}, u32[]{:S(2)}, u32[]{:S(2)}) async-start(bf16[4,320,512]{2,1,0:T(8,128)(2,1)} %bitcast.10), calls=%async_computation | async-start | bytes 2621440 | tf_op jit(solution)/shard_map/all_to_all | solution.py:40
  181.3 107.4 %copy-start.5 = (f32[2652]{0:T(1024)S(1)}, f32[2652]{0:T(1024)}, u32[]{:S(2)}) copy-start(f32[2652]{0:T(1024)} %param.23) | copy-start | bytes 31828
Sparse Core Ops, SparseCore 0:
  8.9 21.2 all-gather.8
  32.3 49.0 all-gather.4
  83.6 47.6 all-gather.6
  133.2 155.4 all-gather.10
